TPU v7x, 32 devices: a whole 2x2x4 slice. The times are simulated.
32 devices in a mesh: ea: 4 (over y, x), row: 4 (over z), col: 2 (over core).
Axes of the slice: x: 2, y: 2, z: 4, core: 2. Of those that a mesh axis runs over, the one named last changes fastest.
Arguments:
- weights: float32 [4, 256, 2048], P('ea', 'row', 'col'), parts along dimension 0, may hold values from -6 to 6
- codebook: float32 [4, 16, 2, 256], P('ea', 'col'), parts along dimension 0, may hold values from -4 to 4
- assign: int32 [4, 256, 1024], P('ea', 'row', 'col'), parts along dimension 0, may hold values from 0 to 255
- chol_upper: float32 [4, 2048, 2048], P('ea', 'row', 'col'), parts along dimension 0, may hold values from 0 to 1.4, as said below
- inv_blocks: float32 [4, 16, 128, 128], P('ea', 'col'), parts along dimension 0, may hold values from -1 to 1.5, as said below
Outputs:
- errors: float32 [4, 256, 2048], P('ea', 'row', 'col'), parts along dimension 0
- row_loss: float32 [4, 256], P('ea', 'row'), parts along dimension 0
- codeword_mass: float32 [4, 16, 256], P('ea', 'col'), parts along dimension 0
There are 4 independent parts, one for each index of `ea`. A program takes and returns all parts, laid end to end along the dimension named above; each array names one. Nothing has to cross between parts.
Inputs may be any that keep to these rules, and one draw needn't show every extreme that they name: `chol_upper`: upper triangular with a positive diagonal. inv_blocks[x, b] is the inverse of the diagonal block of chol_upper[x] on rows and columns [b * 128, (b + 1) * 128).
All inputs are finite; a program needn't handle non-finite values.
Results may differ from a plain program's by a relative error of at most 0.0001.
Values sent between devices are 32-bit elements; how exact they have to be, the bound alone decides.
A program may use at most 64 MiB of HBM per device.

v0:
```python
import jax
import jax.numpy as jnp
from jax import lax
from jax.sharding import PartitionSpec as P


def from_root(value, axis, source):
    kept = jnp.where(lax.axis_index(axis) == source, value, 0).astype(value.dtype)
    return lax.psum(kept, axis)


def flat_labels(assign, half_block, code_count):
    pair_count = assign.shape[2]
    offsets = jnp.arange(pair_count, dtype=jnp.int32) // half_block * code_count
    return assign + offsets[None, None, :]


def lookup_local(codebook, labels):
    experts, row_count, pair_count = labels.shape
    code_table = jnp.transpose(codebook, (0, 2, 1, 3)).reshape(experts, 2, -1)

    def select(rows_table, indices):
        return jnp.stack(
            [jnp.take(rows_table[0], indices), jnp.take(rows_table[1], indices)], axis=-1
        )

    picked = jax.vmap(select)(code_table, labels)
    return picked.reshape(experts, row_count, 2 * pair_count)


def mass_by_code(errors, labels, local_blocks, code_count):
    experts, row_count, width = errors.shape
    squared = errors * errors
    paired = squared.reshape(experts, row_count, width // 2, 2).sum(axis=3)

    def summed(values, marks):
        return jax.ops.segment_sum(
            values.reshape(-1), marks.reshape(-1), num_segments=local_blocks * code_count
        )

    return jax.vmap(summed)(paired, labels).reshape(experts, local_blocks, code_count)


def local(weights, codebook, assign, chol_upper, inv_blocks):
    block_size = inv_blocks.shape[2]
    local_blocks = inv_blocks.shape[1]
    local_width = weights.shape[2]
    code_count = codebook.shape[3]
    column_rank = lax.axis_index("col")
    block_total = local_blocks * lax.axis_size("col")
    labels = flat_labels(assign, block_size // 2, code_count)
    quantized = lookup_local(codebook, labels)
    column_ids = column_rank * local_width + jnp.arange(local_width, dtype=jnp.int32)
    stacked = lax.all_gather(chol_upper, "row", axis=1, tiled=True)

    def panel_of(number):
        return lax.dynamic_slice_in_dim(stacked, number * block_size, block_size, 1)

    def own_block(current, number):
        return lax.dynamic_slice_in_dim(current, number % local_blocks * block_size, block_size, 2)

    def block_error(current_block, number):
        owner_rank = number // local_blocks
        inverse = lax.dynamic_index_in_dim(inv_blocks, number % local_blocks, 1, keepdims=False)
        target = own_block(quantized, number)

        def compute():
            return jnp.einsum(
                "xrc,xcd->xrd", current_block - target, inverse, precision=lax.Precision.HIGHEST
            )

        def nothing():
            return jnp.zeros(current_block.shape, jnp.float32)

        computed = lax.cond(owner_rank == column_rank, compute, nothing)
        return from_root(computed, "col", owner_rank)

    def propagate(current, error_block, panel_rows, number, targets):
        beyond = targets >= (number + 1) * block_size
        masked = jnp.where(beyond[None, None, :], panel_rows, 0.0)
        return current - jnp.einsum(
            "xrc,xcd->xrd", error_block, masked, precision=lax.Precision.HIGHEST
        )

    def record(errors, error_block, number):
        owner_rank = number // local_blocks
        offset = number % local_blocks * block_size
        previous = lax.dynamic_slice_in_dim(errors, offset, block_size, 2)
        chosen = jnp.where(owner_rank == column_rank, error_block, previous)
        return lax.dynamic_update_slice_in_dim(errors, chosen, offset, 2)

    blank = jnp.zeros(weights.shape, jnp.float32)

    def advance(number, state_pair):
        current, errors = state_pair
        error_block = block_error(own_block(current, number), number)
        errors = record(errors, error_block, number)
        current = propagate(current, error_block, panel_of(number), number, column_ids)
        return (current, errors)

    current, errors = lax.fori_loop(0, block_total, advance, (weights, blank))
    row_loss = lax.psum(jnp.sum(errors * errors, axis=2), "col")
    local_mass = mass_by_code(errors, labels, local_blocks, code_count)
    codeword_mass = lax.psum(local_mass, "row")
    return (errors, row_loss, codeword_mass)


def solution(mesh):
    return jax.shard_map(
        local,
        mesh=mesh,
        in_specs=(
            P("ea", "row", "col"),
            P("ea", "col", None, None),
            P("ea", "row", "col"),
            P("ea", "row", "col"),
            P("ea", "col", None, None),
        ),
        out_specs=(P("ea", "row", "col"), P("ea", "row"), P("ea", "col", None)),
        check_vma=False,
    )
```

profile of v0, /device:TPU:1, one launch (start us, length us, event | category | flops | bytes accessed | tf_op | source)
XLA Modules:
  0.0 740.1 jit_solution(10534728693327028452)
XLA Ops:
  9.9 190.2 %gather_fusion.1 = f32[32768]{0:T(1024)S(1)} fusion(f32[1,2048]{1,0:T(1,128)S(1)} %get-tuple-element.332, s32[32768]{0:T(1024)S(1)} %bitcast.50), kind=kCustom, calls=%fused_computation.1.clone | custom fusion | bytes 524288 | tf_op jit(solution)/shard_map/vmap(jit(_take))/gather | solution.py:24
  200.2 190.2 %gather_fusion = f32[32768]{0:T(1024)S(1)} fusion(f32[1,2048]{1,0:T(1,128)S(1)} %get-tuple-element.333, s32[32768]{0:T(1024)S(1)} %bitcast.51), kind=kCustom, calls=%fused_computation.clone | custom fusion | bytes 524288 | tf_op jit(solution)/shard_map/vmap(jit(_take))/gather | solution.py:24
  392.2 98.3 %while.18 = (s32[]{:T(128)}, f32[1,64,1024]{2,1,0:T(8,128)S(1)}, f32[1,64,1024]{2,1,0:T(8,128)S(1)}, s32[]{:T(128)}, f32[1,64,1024]{2,1,0:T(8,128)S(1)}, /*index...) while((s32[]{:T(128)}, f32[1,64,1024]{2,1,0:T(8,128)S(1)}, ...), condition=%wide.region_4.6_spmd.clone, body=%wide.region_0.5_spmd.clone.sunk | while | flops 113477664 | bytes 1477659 | solution.py:101
  392.3 4.3 psum.32
  398.3 4.5 psum.32
  404.5 4.5 psum.32
  409.0 1.5 fusion.35
  410.6 4.5 psum.32
  415.1 1.5 fusion.35
  416.8 4.5 psum.32
  421.3 1.5 fusion.35
  423.0 4.5 psum.32
  427.4 1.5 fusion.35
  429.1 4.5 psum.32
  435.3 4.5 psum.32
  439.8 1.5 fusion.35
  442.5 3.4 psum.32
  445.9 1.5 fusion.35
  448.7 3.4 psum.32
  452.1 1.5 fusion.35
  454.8 3.4 psum.32
  458.2 1.5 fusion.35
  461.0 3.4 psum.32
  467.1 3.4 psum.32
  470.5 1.5 fusion.35
  473.3 3.4 psum.32
  476.7 1.5 fusion.35
  479.4 3.4 psum.32
  485.6 3.4 psum.32
  490.7 3.0 psum.28
  494.7 226.3 %scatter_custom_fusion = f32[2048]{0:T(1024)S(1)} fusion(s32[32768]{0:T(1024)S(1)} %broadcast_select_fusion.1, f32[32768]{0:T(1024)S(1)} %bitcast.55, f32[]{:T(128)} %constant.181.clone.1), kind=kCustom, calls=%fused_computation.45 | custom fusion | flops 32768 | bytes 8196
  721.0 12.2 %psum.29 = f32[1,8,256]{2,1,0:T(8,128)} all-reduce(f32[1,8,256]{2,1,0:T(8,128)S(1)} %reshape.106), channel_id=1, replica_groups=mesh['ea'=4,'row'=4,'col'=2] {'row'}, use_global_device_ids=true, to_apply=%region_9.11 | all-reduce | flops 2048 | bytes 16384 | tf_op jit(solution)/shard_map/psum | solution.py:104
  (121 shorter events, 32.9 us)
Async XLA Ops:
  7.2 385.0 %all-gather.2.cloned.1.call-start = ((), (), s32[]{:S(2)}) async-start(), calls=%async_computation | async-start | bytes 10485760 | tf_op jit(solution)/shard_map/all_gather | solution.py:54
  200.2 190.9 %copy-start.3 = (s32[2]{0:T(128)S(1)}, s32[2]{0:T(128)}, u32[]{:S(2)}) copy-start(s32[2]{0:T(128)} %constant.194) | copy-start | bytes 28
  200.2 191.3 %copy-start.2 = (s32[2]{0:T(128)S(1)}, s32[2]{0:T(128)}, u32[]{:S(2)}) copy-start(s32[2]{0:T(128)} %constant.197) | copy-start | bytes 28
  200.2 192.0 %copy-start = (f32[1,64,1024]{2,1,0:T(8,128)S(1)}, f32[1,64,1024]{2,1,0:T(8,128)}, u32[]{:S(2)}) copy-start(f32[1,64,1024]{2,1,0:T(8,128)} %param.11) | copy-start | bytes 786436
  490.6 242.6 %copy-start.1 = (f32[1,64,1024]{2,1,0:T(8,128)}, f32[1,64,1024]{2,1,0:T(8,128)S(1)}, u32[]{:S(2)}) copy-start(f32[1,64,1024]{2,1,0:T(8,128)S(1)} %get-tuple-element.263) | copy-start | bytes 786436
Sparse Core Ops, SparseCore 0:
  9.5 151.8 all-gather.1
where the time goes:
time: 744 us; the launch traced here: 740 us
  local copies, waits for them, and re-layouts  382 us (51%)
  other arithmetic  230 us (31%)
  blocking collectives  78.1 us (10%)
  matrix products  33 us (4%)
  between operations  14.3 us (2%)
    unnamed x5, other arithmetic  227 us
    gather x3, local copies, waits for them, and re-layouts, select(): jnp.take(rows_table[0], indices)  190 us
    gather x2, local copies, waits for them, and re-layouts, select(): jnp.take(rows_table[1], indices)  190 us
    psum x16, blocking collectives, from_root(): return lax.psum(kept, axis)  63 us
    dot_general x16, matrix products, propagate(): jnp.einsum('xrc,xcd->xrd', error_block, masked, precision=lax.Precision.H...  24.4 us
  transfers between devices with their start and end apart: 1, of which 0 were waited for; matrix products, arithmetic and copies ran while one was open for 52% of the time, Pallas kernels for 0%

commit v1 on v0

v1 whole, which is shorter than its diff:
```python
import functools

import jax
import jax.numpy as jnp
from jax import lax
from jax.experimental import pallas as pl
from jax.experimental.pallas import tpu as pltpu
from jax.sharding import PartitionSpec as P

F32 = jnp.float32
BF16 = jnp.bfloat16
LOW = 16


def halves(value):
    high = value.astype(BF16)
    return high, (value - high.astype(F32)).astype(BF16)


def dot(a, b):
    return jnp.dot(a, b, preferred_element_type=F32)


def dot3(a, b_high, b_low):
    rows = a.shape[0]
    high, low = halves(a)
    both = dot(jnp.concatenate([high, low], axis=0), b_high)
    return both[:rows] + both[rows:] + dot(high, b_low)


def dot_full(a, b):
    b_high, b_low = halves(b)
    return dot3(a, b_high, b_low)


def take(table, index):
    return jnp.take_along_axis(table, index, axis=1, mode="promise_in_bounds")


def kernel(
    nr, nc,
    weights, codebook, assign, inverse, factor,
    errors_out, loss_out, mass_out,
    u_raw, u_high, u_low, v_full, v_high, v_low, delta, codes, delta_in, run_in, run_out,
    err_block, err_own, mass_all, loss_all,
    u_sem, d_send, d_recv, run_send, run_recv, core_send, core_recv, own_send, own_recv,
    mass_send, mass_recv, loss_send, loss_recv,
):
    z = lax.axis_index("row")
    c = lax.axis_index("col")
    rows, width = weights.shape
    span = factor.shape[0]
    m = width // span
    block = inverse.shape[1]
    k = span // block
    code_count = codebook.shape[2]
    owner = z // m
    slot = z % m
    is_owner = c == owner

    def remote(src, dst, send, recv, row, col):
        return pltpu.make_async_remote_copy(
            src_ref=src, dst_ref=dst, send_sem=send, recv_sem=recv,
            device_id={"row": row, "col": col}, device_id_type=pl.DeviceIdType.MESH,
        )

    load = pltpu.make_async_copy(factor, u_raw, u_sem)
    load.start()

    barrier = pltpu.get_barrier_semaphore()
    for step in range(1, nr * nc):
        other = lax.rem(z * nc + c + step, nr * nc)
        pl.semaphore_signal(
            barrier, inc=1, device_id={"row": other // nc, "col": other % nc},
            device_id_type=pl.DeviceIdType.MESH,
        )

    lane = lax.broadcasted_iota(jnp.int32, (rows, block), 1)
    for b in range(width // block):
        first = b * (block // 2)
        tile = first // block * block
        code = take(assign[:, tile:tile + block], first - tile + lane // 2)
        codes[b] = code
        inner = code % block
        value = jnp.zeros((rows, block), F32)
        for part in range(code_count // block):
            picked = []
            for comp in range(2):
                table = codebook[b, comp:comp + 1, part * block:(part + 1) * block]
                picked.append(take(jnp.broadcast_to(table, (rows, block)), inner))
            both = jnp.where(lane % 2 == 0, picked[0], picked[1])
            value = jnp.where(code // block == part, both, value)
        j, at = b * block // span, b * block % span
        delta[j, :, at:at + block] = weights[:, b * block:(b + 1) * block] - value

    @pl.when(z == 0)
    def _():
        run_in[...] = jnp.zeros_like(run_in)

    pl.semaphore_wait(barrier, nr * nc - 1)

    def delta_copy(j):
        return remote(delta.at[j], delta_in.at[z], d_send.at[j], d_recv.at[z], c * m + j, c)

    for j in range(m):
        @pl.when(c * m + j < z)
        def _():
            delta_copy(j).start()

    load.wait()

    @pl.when(is_owner)
    def _():
        v_full[...] = jnp.zeros_like(v_full)
        base = slot * span

        def invert(lo, hi):
            if hi - lo == 1:
                v_full[lo * block:hi * block, lo * block:hi * block] = inverse[slot * k + lo]
                return
            mid = (lo + hi) // 2
            invert(lo, mid)
            invert(mid, hi)
            top, middle, end = lo * block, mid * block, hi * block
            right = u_raw[top:middle, pl.ds(pl.multiple_of(base + middle, block), end - middle)]
            product = dot_full(v_full[top:middle, top:middle], right)
            v_full[top:middle, middle:end] = -dot_full(product, v_full[middle:end, middle:end])

        invert(0, k)
        high, low = halves(v_full[...])
        v_high[...] = high
        v_low[...] = low

    for j in range(m):
        @pl.when(c * m + j > z)
        def _():
            high, low = halves(u_raw[:, j * span:(j + 1) * span])
            u_high[:, j * span:(j + 1) * span] = high
            u_low[:, j * span:(j + 1) * span] = low

    def run_copy(g, j):
        return remote(run_out.at[g, j], run_in.at[g, j], run_send.at[g, j], run_recv.at[g, j], z + 1, c)

    def core_copy(g, col):
        return remote(err_block.at[g], err_block.at[g], core_send.at[g, col], core_recv.at[g], z, col)

    def own_copy(g):
        return remote(err_block.at[g], err_own.at[slot], own_send.at[g], own_recv.at[slot], g, c)

    def arrived(ref, sem):
        pltpu.make_async_copy(ref, ref, sem).wait()

    def stage(g, _):
        @pl.when(is_owner)
        def _():
            @pl.when(z > 0)
            def _():
                arrived(run_in.at[g, slot], run_recv.at[g, slot])

            @pl.when(g > z)
            def _():
                arrived(delta_in.at[g], d_recv.at[g])
                run_in[g, slot] = run_in[g, slot] + delta_in[g]

            @pl.when(g == z)
            def _():
                run_in[g, slot] = run_in[g, slot] + delta[slot]

            error = dot3(run_in[g, slot], v_high[...], v_low[...])
            err_block[g] = error

            @pl.when(g == z)
            def _():
                err_own[slot] = error

            for col in range(1, nc):
                @pl.when(col > c)
                def _():
                    core_copy(g, col).start()

            @pl.when(g != z)
            def _():
                own_copy(g).start()

        @pl.when(c > owner)
        def _():
            arrived(err_block.at[g], core_recv.at[g])

        for j in range(m):
            @pl.when(c * m + j > z)
            def _():
                change = dot3(
                    err_block[g], u_high[:, j * span:(j + 1) * span], u_low[:, j * span:(j + 1) * span]
                )

                @pl.when(z > 0)
                def _():
                    arrived(run_in.at[g, j], run_recv.at[g, j])

                local = jnp.where(g == z, delta[j], 0.0)
                run_out[g, j] = run_in[g, j] + local - change
                run_copy(g, j).start()

        return 0

    lax.fori_loop(0, nr, stage, 0)

    high_count = code_count // LOW
    group = 2 * high_count
    chunk = 8
    loss = jnp.zeros((8, rows), F32)
    for j in range(m):
        @pl.when(c * m + j != z)
        def _():
            arrived(err_own.at[j], own_recv.at[j])

        error = err_own[j]
        errors_out[:, j * span:(j + 1) * span] = error
        squared = error * error
        loss = loss + lax.dot_general(
            jnp.ones((8, span), F32), squared, (((1,), (1,)), ((), ())),
            precision=lax.Precision.HIGHEST, preferred_element_type=F32,
        )

        def gather(step, total):
            at = pl.ds(pl.multiple_of(step * chunk, chunk), chunk)
            iota_high = lax.broadcasted_iota(jnp.int32, (high_count, block), 0)
            iota_low = lax.broadcasted_iota(jnp.int32, (LOW, block), 0)
            left, right = [], []
            for b in range(k):
                code = codes[j * k + b, at, :]
                value = err_own[j, at, b * block:(b + 1) * block]
                value = value * value
                coarse = value.astype(BF16).astype(F32)
                fine = value - coarse
                code_high, code_low = code // LOW, code % LOW
                top, bottom, marks = [], [], []
                for r in range(chunk):
                    hit = jnp.broadcast_to(code_high[r:r + 1], (high_count, block)) == iota_high
                    top.append(jnp.where(hit, jnp.broadcast_to(coarse[r:r + 1], (high_count, block)), 0.0).astype(BF16))
                    bottom.append(jnp.where(hit, jnp.broadcast_to(fine[r:r + 1], (high_count, block)), 0.0).astype(BF16))
                    low_hit = jnp.broadcast_to(code_low[r:r + 1], (LOW, block)) == iota_low
                    marks.append(jnp.where(low_hit, 1.0, 0.0).astype(BF16))
                left += [jnp.concatenate(top, axis=1), jnp.concatenate(bottom, axis=1)]
                right.append(jnp.concatenate(marks, axis=1))
            return total + lax.dot_general(
                jnp.concatenate(left, axis=0), jnp.concatenate(right, axis=0),
                (((1,), (1,)), ((), ())), preferred_element_type=F32,
            )

        total = lax.fori_loop(0, rows // chunk, gather, jnp.zeros((k * group, k * LOW), F32))
        row_id = lax.broadcasted_iota(jnp.int32, total.shape, 0)
        col_id = lax.broadcasted_iota(jnp.int32, total.shape, 1)
        total = jnp.where(row_id // group == col_id // LOW, total, 0.0)
        wide_row = lax.broadcasted_iota(jnp.int32, (k * LOW, code_count), 0)
        wide_col = lax.broadcasted_iota(jnp.int32, (k * LOW, code_count), 1)
        spread = jnp.where(wide_row % LOW == wide_col % LOW, 1.0, 0.0)
        spread = jnp.dot(total, spread, precision=lax.Precision.HIGHEST, preferred_element_type=F32)
        out_row = lax.broadcasted_iota(jnp.int32, spread.shape, 0)
        out_col = lax.broadcasted_iota(jnp.int32, spread.shape, 1)
        spread = jnp.where(out_row % high_count == out_col // LOW, spread, 0.0)
        for b in range(k):
            mass_all[z, j * k + b:j * k + b + 1, :] = jnp.sum(
                spread[b * group:(b + 1) * group], axis=0, keepdims=True
            )

    loss_all[c, :, :rows] = loss

    def mass_copy(row):
        return remote(mass_all.at[z], mass_all.at[z], mass_send.at[row], mass_recv.at[z], row, c)

    def loss_copy(col):
        return remote(loss_all.at[c], loss_all.at[c], loss_send.at[col], loss_recv.at[c], z, col)

    for row in range(nr):
        @pl.when(row != z)
        def _():
            mass_copy(row).start()
    for col in range(nc):
        @pl.when(col != c)
        def _():
            loss_copy(col).start()

    for j in range(m):
        @pl.when(c * m + j < z)
        def _():
            delta_copy(j).wait_send()

    def drain(g, _):
        for j in range(m):
            @pl.when(c * m + j > z)
            def _():
                run_copy(g, j).wait_send()

        @pl.when(is_owner)
        def _():
            for col in range(1, nc):
                @pl.when(col > c)
                def _():
                    core_copy(g, col).wait_send()

            @pl.when(g != z)
            def _():
                own_copy(g).wait_send()

        return 0

    lax.fori_loop(0, nr, drain, 0)

    for col in range(nc):
        @pl.when(col != c)
        def _():
            arrived(loss_all.at[col], loss_recv.at[col])
    loss_sum = loss_all[0, 0:1, :rows]
    for col in range(1, nc):
        loss_sum = loss_sum + loss_all[col, 0:1, :rows]
    loss_out[...] = loss_sum
    for row in range(nr):
        @pl.when(row != z)
        def _():
            arrived(mass_all.at[row], mass_recv.at[row])
    mass_sum = mass_all[0]
    for row in range(1, nr):
        mass_sum = mass_sum + mass_all[row]
    mass_out[...] = mass_sum

    for row in range(nr):
        @pl.when(row != z)
        def _():
            mass_copy(row).wait_send()
    for col in range(nc):
        @pl.when(col != c)
        def _():
            loss_copy(col).wait_send()


def local(nr, nc, weights, codebook, assign, chol_upper, inv_blocks):
    rows, width = weights.shape[1:]
    span = chol_upper.shape[1]
    m = width // span
    blocks, code_count = codebook.shape[1], codebook.shape[3]
    block = inv_blocks.shape[2]
    dma = pltpu.SemaphoreType.DMA
    vmem = pl.BlockSpec(memory_space=pltpu.VMEM)
    errors, loss, mass = pl.pallas_call(
        functools.partial(kernel, nr, nc),
        out_shape=(
            jax.ShapeDtypeStruct((rows, width), F32),
            jax.ShapeDtypeStruct((1, rows), F32),
            jax.ShapeDtypeStruct((blocks, code_count), F32),
        ),
        in_specs=[vmem, vmem, vmem, vmem, pl.BlockSpec(memory_space=pl.ANY)],
        out_specs=(vmem, vmem, vmem),
        scratch_shapes=[
            pltpu.VMEM((span, width), F32),
            pltpu.VMEM((span, width), BF16),
            pltpu.VMEM((span, width), BF16),
            pltpu.VMEM((span, span), F32),
            pltpu.VMEM((span, span), BF16),
            pltpu.VMEM((span, span), BF16),
            pltpu.VMEM((m, rows, span), F32),
            pltpu.VMEM((blocks, rows, block), jnp.int32),
            pltpu.VMEM((nr, rows, span), F32),
            pltpu.VMEM((nr, m, rows, span), F32),
            pltpu.VMEM((nr, m, rows, span), F32),
            pltpu.VMEM((nr, rows, span), F32),
            pltpu.VMEM((m, rows, span), F32),
            pltpu.VMEM((nr, blocks, code_count), F32),
            pltpu.VMEM((nc, 8, max(rows, 128)), F32),
            dma,
            dma((m,)), dma((nr,)),
            dma((nr, m)), dma((nr, m)),
            dma((nr, nc)), dma((nr,)),
            dma((nr,)), dma((m,)),
            dma((nr,)), dma((nr,)),
            dma((nc,)), dma((nc,)),
        ],
        compiler_params=pltpu.CompilerParams(
            collective_id=0, has_side_effects=True, vmem_limit_bytes=48 * 1024 * 1024
        ),
    )(weights[0], codebook[0], assign[0], inv_blocks[0], chol_upper[0])
    return errors[None], loss, mass[None]


def solution(mesh):
    return jax.shard_map(
        functools.partial(local, mesh.shape["row"], mesh.shape["col"]),
        mesh=mesh,
        in_specs=(
            P("ea", "row", "col"),
            P("ea", "col", None, None),
            P("ea", "row", "col"),
            P("ea", "row", "col"),
            P("ea", "col", None, None),
        ),
        out_specs=(P("ea", "row", "col"), P("ea", "row"), P("ea", "col", None)),
        check_vma=False,
    )
```

time: 744 us -> 56.4 us (0.08)
  local copies, waits for them, and re-layouts: 382 us -> 7.01 us
  other arithmetic: 230 us -> 0 us
  blocking collectives: 78.1 us -> 0 us
  Pallas kernels: 0 us -> 48.4 us
  matrix products: 33 us -> 0 us
  between operations: 14.3 us -> 0.65 us
    gather x5 -> x0, local copies, waits for them, and re-layouts: 381 us -> none  [the longest x3 190 us: select(): jnp.take(rows_table[0], indices)]
    unnamed x5 -> x0, other arithmetic: 227 us -> none
    psum x18 -> x0, blocking collectives: 78.1 us -> none  [the longest x16 63 us: from_root(): return lax.psum(kept, axis)]
    pallas_call x0 -> x1, Pallas kernels: none -> 48.4 us  [local(): pl.pallas_call(functools.partial(kernel, nr, nc), out_shape=(jax.ShapeDty...]
    dot_general x24 -> x0, matrix products: 33 us -> none  [the longest x16 24.4 us: propagate(): jnp.einsum('xrc,xcd->xrd', error_block, masked, precision=lax.Precision.H...]
  transfers between devices with their start and end apart: 1 -> 0, of which waited for: 0 -> 0; matrix products, arithmetic and copies ran while one was open for 52% -> 0% of each run, Pallas kernels for 0% -> 0%
where the time goes in v1:
time: 56.4 us; the launch traced here: 56.1 us
  Pallas kernels  48.4 us (86%)
  local copies, waits for them, and re-layouts  7.01 us (12%)
  between operations  0.65 us (1%)
    pallas_call x1, Pallas kernels, local(): pl.pallas_call(functools.partial(kernel, nr, nc), out_shape=(jax.ShapeDty...  48.4 us
    unnamed x13, local copies, waits for them, and re-layouts  7.01 us

profile of v1, /device:TPU:1, one launch (start us, length us, event | category | flops | bytes accessed | tf_op | source)
XLA Modules:
  0.0 56.1 jit_solution(18258926677286918385)
XLA Ops:
  0.6 0.0 copy-start
  0.6 1.6 %copy-done = f32[1,512,1024]{2,1,0:T(8,128)S(1)} copy-done((f32[1,512,1024]{2,1,0:T(8,128)S(1)}, f32[1,512,1024]{2,1,0:T(8,128)}, u32[]{:S(2)}) %copy-start) | copy-done | bytes 2097176
  2.2 0.0 copy-start.1
  2.2 1.0 %copy-done.1 = f32[1,8,128,128]{3,2,1,0:T(8,128)S(1)} copy-done((f32[1,8,128,128]{3,2,1,0:T(8,128)S(1)}, f32[1,8,128,128]{3,2,1,0:T(8,128)}, u32[]{:S(2)}) %copy-start.1) | copy-done | bytes 524312
  3.3 0.0 copy-start.2
  3.3 0.9 %copy-done.2 = f32[1,64,1024]{2,1,0:T(8,128)S(1)} copy-done((f32[1,64,1024]{2,1,0:T(8,128)S(1)}, f32[1,64,1024]{2,1,0:T(8,128)}, u32[]{:S(2)}) %copy-start.2) | copy-done | bytes 262168
  4.2 0.0 copy-start.3
  4.2 0.9 %copy-done.3 = s32[1,64,512]{2,1,0:T(8,128)S(1)} copy-done((s32[1,64,512]{2,1,0:T(8,128)S(1)}, s32[1,64,512]{2,1,0:T(8,128)}, u32[]{:S(2)}) %copy-start.3) | copy-done | bytes 131096
  5.1 0.0 copy-start.4
  5.1 0.7 %copy-done.4 = f32[1,8,2,256]{3,2,1,0:T(2,128)S(1)} copy-done((f32[1,8,2,256]{3,2,1,0:T(2,128)S(1)}, f32[1,8,2,256]{3,2,1,0:T(2,128)}, u32[]{:S(2)}) %copy-start.4) | copy-done | bytes 16408
  5.8 48.4 %shard_map.76 = (f32[64,1024]{1,0:T(8,128)S(1)}, f32[1,64]{1,0:T(1,128)S(1)}, f32[8,256]{1,0:T(8,128)S(1)}) custom-call(f32[64,1024]{1,0:T(8,128)S(1)} %bitcast.9, f32[8,2,256]{2,1,0:T(2,128)S(1)} %bitcast.12, s32[64,512]{1,0:T(8,128)S(1)} %bitcast.11, f32[8,128,128]{2,1,0:T(8,128)S(1)} %bitcast.8, f32[512,1024]{1,0:T(8,128)S(1)} %bitcast.7), custom_call_target="tpu_custom_call" | custom-call | tf_op jit(solution)/shard_map/pallas_call | solution.py:345
  54.3 0.7 %copy.11 = f32[1,64,1024]{2,1,0:T(8,128)} copy(f32[1,64,1024]{2,1,0:T(8,128)S(1)} %bitcast.10) | data formatting | bytes 524288
  55.0 0.5 copy.12
  55.5 0.6 %copy.13 = f32[1,8,256]{2,1,0:T(8,128)} copy(f32[1,8,256]{2,1,0:T(8,128)S(1)} %bitcast.13) | data formatting | bytes 16384
Async XLA Ops:
  0.6 1.6 %copy-start = (f32[1,512,1024]{2,1,0:T(8,128)S(1)}, f32[1,512,1024]{2,1,0:T(8,128)}, u32[]{:S(2)}) copy-start(f32[1,512,1024]{2,1,0:T(8,128)} %param.8) | copy-start | bytes 6291460
  2.2 1.0 %copy-start.1 = (f32[1,8,128,128]{3,2,1,0:T(8,128)S(1)}, f32[1,8,128,128]{3,2,1,0:T(8,128)}, u32[]{:S(2)}) copy-start(f32[1,8,128,128]{3,2,1,0:T(8,128)} %param.9) | copy-start | bytes 1572868
  3.3 0.9 %copy-start.2 = (f32[1,64,1024]{2,1,0:T(8,128)S(1)}, f32[1,64,1024]{2,1,0:T(8,128)}, u32[]{:S(2)}) copy-start(f32[1,64,1024]{2,1,0:T(8,128)} %param.5) | copy-start | bytes 786436
  4.2 0.9 %copy-start.3 = (s32[1,64,512]{2,1,0:T(8,128)S(1)}, s32[1,64,512]{2,1,0:T(8,128)}, u32[]{:S(2)}) copy-start(s32[1,64,512]{2,1,0:T(8,128)} %param.7) | copy-start | bytes 393220
  5.1 0.7 %copy-start.4 = (f32[1,8,2,256]{3,2,1,0:T(2,128)S(1)}, f32[1,8,2,256]{3,2,1,0:T(2,128)}, u32[]{:S(2)}) copy-start(f32[1,8,2,256]{3,2,1,0:T(2,128)} %param.6) | copy-start | bytes 49156

commit v2 on v1

--- a/solution.py
+++ b/solution.py
@@ -39,9 +39,9 @@
 
 def kernel(
     nr, nc,
-    weights, codebook, assign, inverse, factor,
+    weights_hbm, codebook_hbm, assign_hbm, inverse_hbm, factor,
     errors_out, loss_out, mass_out,
-    u_raw, u_high, u_low, v_full, v_high, v_low, delta, codes, delta_in, run_in, run_out,
+    weights, codebook, assign, inverse, u_raw, u_high, u_low, v_full, v_high, v_low, delta, codes, delta_in, run_in, run_out,
     err_block, err_own, mass_all, loss_all,
     u_sem, d_send, d_recv, run_send, run_recv, core_send, core_recv, own_send, own_recv,
     mass_send, mass_recv, loss_send, loss_recv,
@@ -64,8 +64,15 @@
             device_id={"row": row, "col": col}, device_id_type=pl.DeviceIdType.MESH,
         )
 
-    load = pltpu.make_async_copy(factor, u_raw, u_sem)
-    load.start()
+    loads = [
+        pltpu.make_async_copy(source, target, u_sem.at[number])
+        for number, (source, target) in enumerate((
+            (assign_hbm, assign), (codebook_hbm, codebook), (weights_hbm, weights),
+            (inverse_hbm, inverse), (factor, u_raw),
+        ))
+    ]
+    for load in loads:
+        load.start()
 
     barrier = pltpu.get_barrier_semaphore()
     for step in range(1, nr * nc):
@@ -74,6 +81,9 @@
             barrier, inc=1, device_id={"row": other // nc, "col": other % nc},
             device_id_type=pl.DeviceIdType.MESH,
         )
+
+    for load in loads[:3]:
+        load.wait()
 
     lane = lax.broadcasted_iota(jnp.int32, (rows, block), 1)
     for b in range(width // block):
@@ -107,7 +117,8 @@
         def _():
             delta_copy(j).start()
 
-    load.wait()
+    for load in loads[3:]:
+        load.wait()
 
     @pl.when(is_owner)
     def _():
@@ -178,7 +189,7 @@
                 def _():
                     core_copy(g, col).start()
 
-            @pl.when(g != z)
+            @pl.when(g < z)
             def _():
                 own_copy(g).start()
 
@@ -204,6 +215,11 @@
         return 0
 
     lax.fori_loop(0, nr, stage, 0)
+
+    for g in range(1, nr):
+        @pl.when(is_owner & (g > z))
+        def _():
+            own_copy(g).start()
 
     high_count = code_count // LOW
     group = 2 * high_count
@@ -248,7 +264,7 @@
                 (((1,), (1,)), ((), ())), preferred_element_type=F32,
             )
 
-        total = lax.fori_loop(0, rows // chunk, gather, jnp.zeros((k * group, k * LOW), F32))
+        total = lax.fori_loop(0, rows // chunk, gather, jnp.zeros((k * group, k * LOW), F32), unroll=4)
         row_id = lax.broadcasted_iota(jnp.int32, total.shape, 0)
         col_id = lax.broadcasted_iota(jnp.int32, total.shape, 1)
         total = jnp.where(row_id // group == col_id // LOW, total, 0.0)
@@ -349,9 +365,13 @@
             jax.ShapeDtypeStruct((1, rows), F32),
             jax.ShapeDtypeStruct((blocks, code_count), F32),
         ),
-        in_specs=[vmem, vmem, vmem, vmem, pl.BlockSpec(memory_space=pl.ANY)],
+        in_specs=[pl.BlockSpec(memory_space=pl.ANY)] * 5,
         out_specs=(vmem, vmem, vmem),
         scratch_shapes=[
+            pltpu.VMEM(weights.shape[1:], F32),
+            pltpu.VMEM(codebook.shape[1:], F32),
+            pltpu.VMEM(assign.shape[1:], jnp.int32),
+            pltpu.VMEM(inv_blocks.shape[1:], F32),
             pltpu.VMEM((span, width), F32),
             pltpu.VMEM((span, width), BF16),
             pltpu.VMEM((span, width), BF16),
@@ -367,7 +387,7 @@
             pltpu.VMEM((m, rows, span), F32),
             pltpu.VMEM((nr, blocks, code_count), F32),
             pltpu.VMEM((nc, 8, max(rows, 128)), F32),
-            dma,
+            dma((5,)),
             dma((m,)), dma((nr,)),
             dma((nr, m)), dma((nr, m)),
             dma((nr, nc)), dma((nr,)),
@@ -376,7 +396,7 @@
             dma((nc,)), dma((nc,)),
         ],
         compiler_params=pltpu.CompilerParams(
-            collective_id=0, has_side_effects=True, vmem_limit_bytes=48 * 1024 * 1024
+            collective_id=0, has_side_effects=True, vmem_limit_bytes=62 * 1024 * 1024
         ),
     )(weights[0], codebook[0], assign[0], inv_blocks[0], chol_upper[0])
     return errors[None], loss, mass[None]

time: 56.4 us -> 52.7 us (0.934)
  local copies, waits for them, and re-layouts: 7.01 us -> 4.05 us
  Pallas kernels: 48.4 us -> 47.8 us
    unnamed x13 -> x3, local copies, waits for them, and re-layouts: 7.01 us -> 4.05 us
    pallas_call x1, Pallas kernels: 48.4 us -> 47.8 us  [local(): pl.pallas_call(functools.partial(kernel, nr, nc), out_shape=(jax.ShapeDty...]
where the time goes in v2:
time: 52.7 us; the launch traced here: 52.5 us
  Pallas kernels  47.8 us (91%)
  local copies, waits for them, and re-layouts  4.05 us (8%)
  between operations  0.64 us (1%)
    pallas_call x1, Pallas kernels, local(): pl.pallas_call(functools.partial(kernel, nr, nc), out_shape=(jax.ShapeDty...  47.8 us
    unnamed x3, local copies, waits for them, and re-layouts  4.05 us

profile of v2, /device:TPU:1, one launch (start us, length us, event | category | flops | bytes accessed | tf_op | source)
XLA Modules:
  0.0 52.5 jit_solution(4464527533808497488)
XLA Ops:
  0.6 47.8 %shard_map.76 = (f32[64,1024]{1,0:T(8,128)}, f32[1,64]{1,0:T(1,128)}, f32[8,256]{1,0:T(8,128)}) custom-call(f32[64,1024]{1,0:T(8,128)} %bitcast.9, f32[8,2,256]{2,1,0:T(2,128)} %bitcast.12, s32[64,512]{1,0:T(8,128)} %bitcast.11, f32[8,128,128]{2,1,0:T(8,128)} %bitcast.8, f32[512,1024]{1,0:T(8,128)} %bitcast.7), custom_call_target="tpu_custom_call" | custom-call | tf_op jit(solution)/shard_map/pallas_call | solution.py:361
  48.5 1.7 %copy.11 = f32[1,64,1024]{2,1,0:T(8,128)} copy(f32[1,64,1024]{2,1,0:T(8,128)} %bitcast.10) | data formatting | bytes 524288
  50.1 1.1 %copy.12 = f32[1,64]{1,0:T(1,128)} copy(f32[1,64]{1,0:T(1,128)} %get-tuple-element.13) | data formatting | bytes 512
  51.2 1.3 %copy.13 = f32[1,8,256]{2,1,0:T(8,128)} copy(f32[1,8,256]{2,1,0:T(8,128)} %bitcast.13) | data formatting | bytes 16384

commit v3 on v2

--- a/solution.py
+++ b/solution.py
@@ -10,6 +10,7 @@
 F32 = jnp.float32
 BF16 = jnp.bfloat16
 LOW = 16
+PIECES = 2
 
 
 def halves(value):
@@ -56,6 +57,8 @@
     code_count = codebook.shape[2]
     owner = z // m
     slot = z % m
+    steps = nr * PIECES
+    piece = rows // PIECES
     is_owner = c == owner
 
     def remote(src, dst, send, recv, row, col):
@@ -155,71 +158,83 @@
     def core_copy(g, col):
         return remote(err_block.at[g], err_block.at[g], core_send.at[g, col], core_recv.at[g], z, col)
 
-    def own_copy(g):
-        return remote(err_block.at[g], err_own.at[slot], own_send.at[g], own_recv.at[slot], g, c)
+    def part_rows(q):
+        return pl.ds(pl.multiple_of(q % PIECES * piece, piece), piece)
+
+    def own_copy(q):
+        return remote(
+            err_block.at[q], err_own.at[slot, part_rows(q)],
+            own_send.at[q], own_recv.at[slot, q % PIECES], q // PIECES, c,
+        )
 
     def arrived(ref, sem):
         pltpu.make_async_copy(ref, ref, sem).wait()
 
-    def stage(g, _):
+    def stage(q, _):
+        g = q // PIECES
+        at = part_rows(q)
+
         @pl.when(is_owner)
         def _():
             @pl.when(z > 0)
             def _():
-                arrived(run_in.at[g, slot], run_recv.at[g, slot])
+                arrived(run_in.at[q, slot], run_recv.at[q, slot])
 
             @pl.when(g > z)
             def _():
-                arrived(delta_in.at[g], d_recv.at[g])
-                run_in[g, slot] = run_in[g, slot] + delta_in[g]
+                @pl.when(q % PIECES == 0)
+                def _():
+                    arrived(delta_in.at[g], d_recv.at[g])
+
+                run_in[q, slot] = run_in[q, slot] + delta_in[g, at]
 
             @pl.when(g == z)
             def _():
-                run_in[g, slot] = run_in[g, slot] + delta[slot]
-
-            error = dot3(run_in[g, slot], v_high[...], v_low[...])
-            err_block[g] = error
+                run_in[q, slot] = run_in[q, slot] + delta[slot, at]
+
+            error = dot3(run_in[q, slot], v_high[...], v_low[...])
+            err_block[q] = error
 
             @pl.when(g == z)
             def _():
-                err_own[slot] = error
+                err_own[slot, at] = error
 
             for col in range(1, nc):
                 @pl.when(col > c)
                 def _():
-                    core_copy(g, col).start()
+                    core_copy(q, col).start()
 
             @pl.when(g < z)
             def _():
-                own_copy(g).start()
+                own_copy(q).start()
 
         @pl.when(c > owner)
         def _():
-            arrived(err_block.at[g], core_recv.at[g])
+            arrived(err_block.at[q], core_recv.at[q])
 
         for j in range(m):
             @pl.when(c * m + j > z)
             def _():
                 change = dot3(
-                    err_block[g], u_high[:, j * span:(j + 1) * span], u_low[:, j * span:(j + 1) * span]
+                    err_block[q], u_high[:, j * span:(j + 1) * span], u_low[:, j * span:(j + 1) * span]
                 )
 
                 @pl.when(z > 0)
                 def _():
-                    arrived(run_in.at[g, j], run_recv.at[g, j])
-
-                local = jnp.where(g == z, delta[j], 0.0)
-                run_out[g, j] = run_in[g, j] + local - change
-                run_copy(g, j).start()
+                    arrived(run_in.at[q, j], run_recv.at[q, j])
+
+                local = jnp.where(g == z, delta[j, at], 0.0)
+                run_out[q, j] = run_in[q, j] + local - change
+                run_copy(q, j).start()
 
         return 0
 
-    lax.fori_loop(0, nr, stage, 0)
-
-    for g in range(1, nr):
-        @pl.when(is_owner & (g > z))
-        def _():
-            own_copy(g).start()
+    lax.fori_loop(0, steps, stage, 0)
+
+    for q in range(PIECES, steps):
+        @pl.when(is_owner & (q // PIECES > z))
+        def _():
+            own_copy(q).start()
 
     high_count = code_count // LOW
     group = 2 * high_count
@@ -228,7 +243,8 @@
     for j in range(m):
         @pl.when(c * m + j != z)
         def _():
-            arrived(err_own.at[j], own_recv.at[j])
+            for h in range(PIECES):
+                arrived(err_own.at[j, h * piece:(h + 1) * piece], own_recv.at[j, h])
 
         error = err_own[j]
         errors_out[:, j * span:(j + 1) * span] = error
@@ -302,26 +318,26 @@
         def _():
             delta_copy(j).wait_send()
 
-    def drain(g, _):
+    def drain(q, _):
         for j in range(m):
             @pl.when(c * m + j > z)
             def _():
-                run_copy(g, j).wait_send()
+                run_copy(q, j).wait_send()
 
         @pl.when(is_owner)
         def _():
             for col in range(1, nc):
                 @pl.when(col > c)
                 def _():
-                    core_copy(g, col).wait_send()
-
-            @pl.when(g != z)
-            def _():
-                own_copy(g).wait_send()
+                    core_copy(q, col).wait_send()
+
+            @pl.when(q // PIECES != z)
+            def _():
+                own_copy(q).wait_send()
 
         return 0
 
-    lax.fori_loop(0, nr, drain, 0)
+    lax.fori_loop(0, steps, drain, 0)
 
     for col in range(nc):
         @pl.when(col != c)
@@ -354,6 +370,7 @@
     rows, width = weights.shape[1:]
     span = chol_upper.shape[1]
     m = width // span
+    steps, piece = nr * PIECES, rows // PIECES
     blocks, code_count = codebook.shape[1], codebook.shape[3]
     block = inv_blocks.shape[2]
     dma = pltpu.SemaphoreType.DMA
@@ -381,17 +398,17 @@
             pltpu.VMEM((m, rows, span), F32),
             pltpu.VMEM((blocks, rows, block), jnp.int32),
             pltpu.VMEM((nr, rows, span), F32),
-            pltpu.VMEM((nr, m, rows, span), F32),
-            pltpu.VMEM((nr, m, rows, span), F32),
-            pltpu.VMEM((nr, rows, span), F32),
+            pltpu.VMEM((steps, m, piece, span), F32),
+            pltpu.VMEM((steps, m, piece, span), F32),
+            pltpu.VMEM((steps, piece, span), F32),
             pltpu.VMEM((m, rows, span), F32),
             pltpu.VMEM((nr, blocks, code_count), F32),
             pltpu.VMEM((nc, 8, max(rows, 128)), F32),
             dma((5,)),
             dma((m,)), dma((nr,)),
-            dma((nr, m)), dma((nr, m)),
-            dma((nr, nc)), dma((nr,)),
-            dma((nr,)), dma((m,)),
+            dma((steps, m)), dma((steps, m)),
+            dma((steps, nc)), dma((steps,)),
+            dma((steps,)), dma((m, PIECES)),
             dma((nr,)), dma((nr,)),
             dma((nc,)), dma((nc,)),
         ],

time: 52.7 us -> 51.6 us (0.979)
  Pallas kernels: 47.8 us -> 46.7 us
    pallas_call x1, Pallas kernels: 47.8 us -> 46.7 us  [local(): pl.pallas_call(functools.partial(kernel, nr, nc), out_shape=(jax.ShapeDty...]
where the time goes in v3:
time: 51.6 us; the launch traced here: 51.4 us
  Pallas kernels  46.7 us (91%)
  local copies, waits for them, and re-layouts  4.05 us (8%)
  between operations  0.64 us (1%)
    pallas_call x1, Pallas kernels, local(): pl.pallas_call(functools.partial(kernel, nr, nc), out_shape=(jax.ShapeDty...  46.7 us
    unnamed x3, local copies, waits for them, and re-layouts  4.05 us

profile of v3, /device:TPU:1, one launch (start us, length us, event | category | flops | bytes accessed | tf_op | source)
XLA Modules:
  0.0 51.4 jit_solution(12532777958247598898)
XLA Ops:
  0.6 46.7 %shard_map.76 = (f32[64,1024]{1,0:T(8,128)}, f32[1,64]{1,0:T(1,128)}, f32[8,256]{1,0:T(8,128)}) custom-call(f32[64,1024]{1,0:T(8,128)} %bitcast.9, f32[8,2,256]{2,1,0:T(2,128)} %bitcast.12, s32[64,512]{1,0:T(8,128)} %bitcast.11, f32[8,128,128]{2,1,0:T(8,128)} %bitcast.8, f32[512,1024]{1,0:T(8,128)} %bitcast.7), custom_call_target="tpu_custom_call" | custom-call | tf_op jit(solution)/shard_map/pallas_call | solution.py:378
  47.4 1.7 %copy.11 = f32[1,64,1024]{2,1,0:T(8,128)} copy(f32[1,64,1024]{2,1,0:T(8,128)} %bitcast.10) | data formatting | bytes 524288
  49.0 1.1 %copy.12 = f32[1,64]{1,0:T(1,128)} copy(f32[1,64]{1,0:T(1,128)} %get-tuple-element.13) | data formatting | bytes 512
  50.1 1.3 %copy.13 = f32[1,8,256]{2,1,0:T(8,128)} copy(f32[1,8,256]{2,1,0:T(8,128)} %bitcast.13) | data formatting | bytes 16384
